TPU v7x, 128 devices: a whole 4x4x4 slice. The times are simulated.
128 devices in a mesh: seq: 32 (over x_lo, y, z), tensor: 4 (over x_hi, core).
Axes of the slice: x: 4 (x_hi: 2, x_lo: 2; x = x_hi * 2 + x_lo), y: 4, z: 4, core: 2. Of those that a mesh axis runs over, the one named last changes fastest.
Arguments:
- tokens: bfloat16 [8192, 1024], P('seq'), may hold values from -6 to 6
- w_attn: bfloat16 [2, 1024, 3, 1024], P(None, None, None, 'tensor'), may hold values from -0.1875 to 0.1875
- w_out: bfloat16 [2, 1024, 1024], P(None, None, 'tensor'), may hold values from -0.1875 to 0.1875
- w_up: bfloat16 [2, 1024, 4096], P(None, None, 'tensor'), may hold values from -0.1875 to 0.1875
- w_down: bfloat16 [2, 1024, 4096], P(None, None, 'tensor'), may hold values from -0.09375 to 0.09375
- w_head: bfloat16 [256, 1024], replicated, may hold values from -0.1875 to 0.1875
- gains: float32 [5, 1024], replicated, may hold values from 0.1 to 1.9
- q_cotangent: float32 [8192, 256], P('seq'), may hold values from -0.09 to 0.09
- bounds: int32 [32], P('seq'), may hold values from 1 to 256
- resets: int32 [32], P('seq'), may hold values 0 or 1
Outputs:
- q_values: float32 [8192, 256], P('seq')
- grad_attn: float32 [2, 1024, 3, 1024], P(None, 'seq', None, 'tensor')
- grad_out: float32 [2, 1024, 1024], P(None, 'seq', 'tensor')
- grad_up: float32 [2, 1024, 4096], P(None, 'seq', 'tensor')
- grad_down: float32 [2, 1024, 4096], P(None, 'seq', 'tensor')
- grad_head: float32 [256, 1024], P(None, 'seq')
- grad_gains: float32 [5, 1024], P(None, 'seq')
All inputs are finite; a program needn't handle non-finite values. No bound on the sum of `resets` on one device may be relied on, other than what follows from the above.
Results may differ from a plain program's by a relative error of at most 0.033.
Values may be sent and summed in bfloat16 or wider, within the bound.
A program may use at most 128 MiB of HBM per device.

v0:
```python
import functools
import types

import jax
import jax.numpy as jnp
from jax import lax
from jax.experimental import pallas as pl
from jax.experimental.pallas import tpu as pltpu
from jax.sharding import PartitionSpec as P

F32 = jnp.float32
BF16 = jnp.bfloat16
EPS = 1e-06
LAYERS = 2
D = 1024
SEG = 256
HD = 128
CUBIC = 0.044715
ROOT = 0.7978845608028654
MESH = pl.DeviceIdType.MESH
UNITS = 24
NARROW = 3


def nn(a, b):
    return lax.dot_general(a, b, (((1,), (0,)), ((), ())), preferred_element_type=F32)


def nt(a, b):
    return lax.dot_general(a, b, (((1,), (1,)), ((), ())), preferred_element_type=F32)


def tn(a, b):
    return lax.dot_general(a, b, (((0,), (0,)), ((), ())), preferred_element_type=F32)


def loop(count, f):
    def step(i, carry):
        f(i)
        return carry

    lax.fori_loop(0, count, step, 0)


def span(i, size):
    return pl.ds(pl.multiple_of(i * size, size), size)


def near(v):
    return v + 1 - 2 * lax.rem(v, 2)


def far(v):
    return 3 - v


INPUTS = ("tokens", "wa", "wo", "wu", "wd", "wh", "gains", "qcot", "bound", "reset")
OUTPUTS = ("oz", "oe")


def scratch():
    v = pltpu.VMEM
    dma = pltpu.SemaphoreType.DMA
    return dict(
        wA=v((2, 3, D, 256), BF16),
        wO=v((2, D, 256), BF16),
        wU=v((2, D, D), BF16),
        wD=v((2, D, D), BF16),
        wH=v((256, D), BF16),
        h=v((3, SEG, D), BF16),
        a=v((2, 2 * SEG, D), BF16),
        q=v((2, SEG, 256), BF16),
        k=v((2, 2 * SEG, 256), BF16),
        v=v((2, 2 * SEG, 256), BF16),
        p=v((2, 2, SEG, 2 * SEG), F32),
        ctx=v((2, SEG, 256), BF16),
        mid=v((2, SEG, D), BF16),
        b=v((2, SEG, D), BF16),
        slope=v((2, SEG, D), F32),
        act=v((2, SEG, D), BF16),
        ar_send=v((128, D), BF16),
        ar_half=v((2, 128, D), BF16),
        ar_sum=v((128, D), BF16),
        ar_far=v((2, 128, D), BF16),
        ar_own=v((128, D), F32),
        db=v((SEG, D), BF16),
        dh=v((SEG, D), F32),
        xt=v((D, 2 * SEG), BF16),
        final=v((SEG, D), BF16),
        dy=v((SEG, D), BF16),
        dup=v((SEG, D), BF16),
        dctx=v((SEG, 256), BF16),
        dqs=v((SEG, 256), BF16),
        dkv=v((2, 2 * SEG, 256), BF16),
        wide_tmp=v((SEG, D), F32),
        gg=v((5, 8, D), F32),
        g0=v((2, 8, D), F32),
        g0s=v((8, D), F32),
        bs=v((8, 256), jnp.int32),
        br=v((8, 256), jnp.int32),
        G=v((UNITS, 2, 4, 4, 32, 256), BF16),
        R1=v((UNITS, 2, 2, 4, 32, 256), BF16),
        R2=v((UNITS, 2, 4, 32, 256), BF16),
        R3=v((UNITS, 2, 2, 32, 256), BF16),
        R4=v((UNITS, 2, 32, 256), BF16),
        R5=v((UNITS, 32, 256), BF16),
        G_=v((NARROW, 2, 4, 4, 32, 128), BF16),
        R1_=v((NARROW, 2, 2, 4, 32, 128), BF16),
        R2_=v((NARROW, 2, 4, 32, 128), BF16),
        R3_=v((NARROW, 2, 2, 32, 128), BF16),
        R4_=v((NARROW, 2, 32, 128), BF16),
        R5_=v((NARROW, 32, 128), BF16),
        w_sem=dma((10,)),
        ar_s=dma((7, 3)),
        ar_r=dma((7, 3)),
        kv_s=dma((2, 2)),
        kv_r=dma((2, 2)),
        pa_s=dma((2, 2)),
        pa_r=dma((2, 2)),
        b_s=dma,
        b_r=dma,
        g0_s=dma((2,)),
        g0_r=dma((2,)),
        rs_s=dma((UNITS + NARROW, 7)),
        rs_r=dma((UNITS + NARROW, 7)),
    )


COLORS = (("y", 0, 0), ("z", 0, 0), ("y", 1, 1), ("z", 1, 1))


class Share:
    def __init__(self, r, here, index, narrow, color, write):
        tail = "_" if narrow else ""
        self.g, self.r1, self.r2, self.r3, self.r4, self.r5 = (
            getattr(r, name + tail).at[index] for name in ("G", "R1", "R2", "R3", "R4", "R5")
        )
        row = index + (UNITS if narrow else 0)
        self.ss = [r.rs_s.at[row, n] for n in range(7)]
        self.rs = [r.rs_r.at[row, n] for n in range(7)]
        self.here = here
        self.axis, o1, o2 = color
        self.f1, self.f2 = (far, near) if o1 else (near, far)
        self.e1, self.e2 = (far, near) if o2 else (near, far)
        self.write = write
        self.stage = 0

    def one(self, value):
        return self.g.at[:, value] if self.axis == "y" else self.g.at[:, :, value]

    def two(self, value):
        if self.axis == "y":
            return self.g.at[:, self.here.y, value]
        return self.g.at[:, value, self.here.z]

    def device(self, first=None, second=None, x=None):
        h = self.here
        y, z = h.y, h.z
        if first is not None:
            y, z = (first, z) if self.axis == "y" else (y, first)
        if second is not None:
            y, z = (y, second) if self.axis == "y" else (second, z)
        x = h.x if x is None else x
        return (x * 16 + y * 4 + z, h.t)

    def send(self, n, source, target, device):
        copy = pltpu.make_async_remote_copy(
            src_ref=source,
            dst_ref=target,
            send_sem=self.ss[n],
            recv_sem=self.rs[n],
            device_id=device,
            device_id_type=MESH,
        )
        copy.start()
        return copy

    def advance(self):
        h = self.here
        v, w = (h.y, h.z) if self.axis == "y" else (h.z, h.y)
        stage = self.stage
        if stage > 5:
            return
        self.stage += 1
        if stage == 0:
            peer = self.f1(v)
            to = self.device(first=peer)
            self.c = [
                self.send(0, self.one(peer), self.r1.at[0], to),
                self.send(1, self.one(self.f2(peer)), self.r1.at[1], to),
            ]
            return
        for copy in self.c:
            copy.wait()
        if stage == 1:
            peer = self.f2(v)
            part = self.one(peer)
            part[...] = (part[...].astype(F32) + self.r1[1].astype(F32)).astype(BF16)
            self.c = [self.send(2, part, self.r2, self.device(first=peer))]
        elif stage == 2:
            part = self.one(v)
            part[...] = (
                part[...].astype(F32) + self.r1[0].astype(F32) + self.r2[...].astype(F32)
            ).astype(BF16)
            peer = self.e1(w)
            to = self.device(second=peer)
            self.c = [
                self.send(3, self.two(peer), self.r3.at[0], to),
                self.send(4, self.two(self.e2(peer)), self.r3.at[1], to),
            ]
        elif stage == 3:
            peer = self.e2(w)
            part = self.two(peer)
            part[...] = (part[...].astype(F32) + self.r3[1].astype(F32)).astype(BF16)
            self.c = [self.send(5, part, self.r4, self.device(second=peer))]
        elif stage == 4:
            part = self.two(w)
            part[...] = (
                part[...].astype(F32) + self.r3[0].astype(F32) + self.r4[...].astype(F32)
            ).astype(BF16)
            other = self.g.at[1 - h.x, h.y, h.z]
            self.c = [self.send(6, other, self.r5, self.device(x=1 - h.x))]
        else:
            own = self.g[h.x, h.y, h.z]
            self.write(own.astype(F32) + self.r5[...].astype(F32))


def norm_vjp(x, gain, dy):
    r = lax.rsqrt(jnp.mean(x * x, axis=-1, keepdims=True) + EPS)
    scaled = dy * gain
    inner = jnp.mean(scaled * x, axis=-1, keepdims=True)
    dx = r * scaled - x * (r * r * r * inner)
    return dx, dy * (x * r)


def kernel(*refs):
    scratches = scratch()
    r = types.SimpleNamespace(**dict(zip(INPUTS + OUTPUTS + tuple(scratches), refs)))
    s = lax.axis_index("seq")
    t = lax.axis_index("tensor")
    here = types.SimpleNamespace(
        x=lax.div(s, 16), y=lax.rem(lax.div(s, 4), 4), z=lax.rem(s, 4), t=t, s=s
    )
    core, chip = lax.rem(t, 2), lax.div(t, 2)
    beside = (s, chip * 2 + 1 - core)
    across = (s, (1 - chip) * 2 + core)
    following = (lax.rem(s + 1, 32), t)
    preceding = (lax.rem(s + 31, 32), t)
    at = lambda x, y, z: (x * 16 + y * 4 + z, t)
    peers = [
        beside,
        across,
        following,
        preceding,
        at(1 - here.x, here.y, here.z),
        at(here.x, near(here.y), here.z),
        at(here.x, far(here.y), here.z),
        at(here.x, here.y, near(here.z)),
        at(here.x, here.y, far(here.z)),
    ]

    loads = {}
    order = [("tok", r.tokens, r.h.at[0])]
    for l in range(LAYERS):
        order.append((("A", l), r.wa.at[l], r.wA.at[l]))
        order.append((("O", l), r.wo.at[l], r.wO.at[l]))
        order.append((("U", l), r.wu.at[l], r.wU.at[l]))
        order.append((("D", l), r.wd.at[l], r.wD.at[l]))
    order.append(("H", r.wh, r.wH))
    for n, (name, source, target) in enumerate(order):
        loads[name] = pltpu.make_async_copy(source, target, r.w_sem.at[n])
        if n < 2:
            loads[name].start()

    barrier = pltpu.get_barrier_semaphore()
    for peer in peers:
        pl.semaphore_signal(barrier, inc=1, device_id=peer, device_id_type=MESH)
    r.gg[...] = jnp.zeros_like(r.gg)
    bound = r.bound[0]
    restart = jnp.where(s == 0, 1, r.reset[0])
    r.bs[...] = jnp.full((8, 256), bound, jnp.int32)

    def remote(source, target, send_sem, recv_sem, device):
        return pltpu.make_async_remote_copy(
            src_ref=source,
            dst_ref=target,
            send_sem=send_sem,
            recv_sem=recv_sem,
            device_id=device,
            device_id_type=MESH,
        )

    def norm_into(source, k, target):
        def rows(i):
            block = span(i, 64)
            x = source[block, :].astype(F32)
            scale = lax.rsqrt(jnp.mean(x * x, axis=-1, keepdims=True) + EPS)
            target[block, :] = (x * scale * r.gains[k : k + 1, :]).astype(BF16)

        loop(4, rows)

    def ar_begin(n, part):
        base = (1 - core) * 128

        def first(i):
            r.ar_send[:, span(i, 256)] = part(base, i).astype(BF16)

        loop(4, first)
        half = r.ar_half.at[n % 2]
        copy = remote(r.ar_send, half, r.ar_s.at[n, 0], r.ar_r.at[n, 0], beside)
        copy.start()

        def second(i):
            r.ar_own[:, span(i, 256)] = part(core * 128, i)

        loop(4, second)
        copy.wait()
        r.ar_sum[...] = (r.ar_own[...] + half[...].astype(F32)).astype(BF16)
        copy = remote(
            r.ar_sum, r.ar_far.at[n % 2], r.ar_s.at[n, 1], r.ar_r.at[n, 1], across
        )
        copy.start()
        return copy

    def ar_end(n, copy, target, residual):
        copy.wait()
        mine = pl.ds(pl.multiple_of(core * 128, 128), 128)
        total = r.ar_sum[...].astype(F32) + r.ar_far[n % 2].astype(F32)
        if residual is not None:
            total = residual[mine, :].astype(F32) + total
        target[mine, :] = total.astype(BF16)
        copy = remote(
            target.at[mine, :], target.at[mine, :], r.ar_s.at[n, 2], r.ar_r.at[n, 2], beside
        )
        copy.start()
        copy.wait()

    def at_rows(base):
        return pl.ds(pl.multiple_of(base, 128), 128)

    loads["tok"].wait()
    own = pl.ds(SEG, SEG)
    for l in range(LAYERS):
        h, a, q, k, v = r.h.at[l], r.a.at[l, own], r.q.at[l], r.k.at[l], r.v.at[l]
        norm_into(h, 2 * l, a)
        loads["A", l].wait()
        if l == 0:
            for name, _, _ in order[2:]:
                loads[name].start()
        k[own, :] = nn(a[...], r.wA[l, 1]).astype(BF16)
        if l == 0:
            pl.semaphore_wait(barrier, len(peers))
            bound_copy = remote(r.bs, r.br, r.b_s, r.b_r, following)
            bound_copy.start()
        send_k = remote(
            k.at[own], k.at[pl.ds(0, SEG)], r.kv_s.at[l, 0], r.kv_r.at[l, 0], following
        )
        send_k.start()
        v[own, :] = nn(a[...], r.wA[l, 2]).astype(BF16)
        send_v = remote(
            v.at[own], v.at[pl.ds(0, SEG)], r.kv_s.at[l, 1], r.kv_r.at[l, 1], following
        )
        send_v.start()
        q[...] = nn(a[...], r.wA[l, 0]).astype(BF16)
        for head in range(2):
            lanes = slice(head * HD, (head + 1) * HD)

            def local(i):
                block = span(i, 128)
                scores = nt(q[block, lanes], k[own, lanes]) * (HD**-0.5)
                row = lax.broadcasted_iota(jnp.int32, (128, SEG), 0) + i * 128
                col = lax.broadcasted_iota(jnp.int32, (128, SEG), 1)
                allowed = (col <= row) & ((col >= bound) | (row < bound))
                r.p[l, head, block, own] = jnp.where(allowed, jnp.exp(scores), 0.0)

            loop(2, local)
        if l == 0:
            bound_copy.wait()
        send_k.wait()
        for head in range(2):
            lanes = slice(head * HD, (head + 1) * HD)

            def memory(i):
                block = span(i, 128)
                scores = nt(q[block, lanes], k[0:SEG, lanes]) * (HD**-0.5)
                row = lax.broadcasted_iota(jnp.int32, (128, SEG), 0) + i * 128
                col = lax.broadcasted_iota(jnp.int32, (128, SEG), 1)
                prior = lax.rem(r.br[0:1, :], SEG)
                allowed = (row < bound) & (restart == 0) & (col >= prior)
                e = jnp.where(allowed, jnp.exp(scores), 0.0)
                e_own = r.p[l, head, block, own]
                total = jnp.sum(e + e_own, axis=-1, keepdims=True)
                r.p[l, head, block, 0:SEG] = e / total
                r.p[l, head, block, own] = e_own / total

            loop(2, memory)
        send_v.wait()
        prev = r.a.at[l, at_rows(core * 128)]
        send_a = remote(
            r.a.at[l, at_rows(SEG + core * 128)],
            prev,
            r.pa_s.at[l, 0],
            r.pa_r.at[l, 0],
            following,
        )
        send_a.start()
        for head in range(2):
            lanes = slice(head * HD, (head + 1) * HD)

            def attend(i):
                block = span(i, 128)
                probs = r.p[l, head, block, :].astype(BF16)
                r.ctx[l, block, lanes] = nn(probs, v[:, lanes]).astype(BF16)

            loop(2, attend)
        loads["O", l].wait()
        copy = ar_begin(
            2 * l, lambda base, i: nt(r.ctx[l, at_rows(base), :], r.wO[l, span(i, 256), :])
        )
        ar_end(2 * l, copy, r.mid.at[l], h)
        norm_into(r.mid.at[l], 2 * l + 1, r.b.at[l])
        loads["U", l].wait()

        def upper(i):
            lanes = span(i, 256)
            u = nn(r.b[l], r.wU[l, :, lanes])
            th = jnp.tanh(ROOT * (u + CUBIC * (u * u * u)))
            half = 0.5 * (1.0 + th)
            r.act[l, :, lanes] = (u * half).astype(BF16)
            r.slope[l, :, lanes] = half + (0.5 * ROOT) * u * (1.0 - th * th) * (
                1.0 + (3.0 * CUBIC) * (u * u)
            )

        loop(4, upper)
        loads["D", l].wait()
        copy = ar_begin(
            2 * l + 1,
            lambda base, i: nt(r.act[l, at_rows(base), :], r.wD[l, span(i, 256), :]),
        )
        send_a.wait()
        share_a = remote(prev, prev, r.pa_s.at[l, 1], r.pa_r.at[l, 1], beside)
        share_a.start()
        ar_end(2 * l + 1, copy, r.h.at[l + 1], r.mid.at[l])
        share_a.wait()

    def transposed(source):
        count = source.shape[0]

        def cols(i):
            lanes = span(i, 256)
            r.xt[lanes, 0:count] = source[:, lanes].T

        loop(4, cols)

    def outer(g, value):
        g[...] = value.astype(BF16).reshape(g.shape)

    def share(index, narrow, color, write):
        return Share(r, here, index, narrow, COLORS[color], write)

    def wide(index, color, left, write):
        unit = share(index, False, color, write)
        outer(unit.g, left())
        unit.advance()
        return unit

    def step(units):
        for unit in units:
            unit.advance()

    def norm_back(source, k, dy_of, add):
        def rows(i):
            block = span(i, 64)
            dx, dg = norm_vjp(source[block, :].astype(F32), r.gains[k : k + 1, :], dy_of(block))
            r.dh[block, :] = (r.dh[block, :] + dx) if add else dx
            r.gg[k] += jnp.sum(dg.reshape(8, 8, D), axis=0)

        loop(4, rows)

    def rounded_dh():
        def rows(i):
            block = span(i, 64)
            r.dy[block, :] = r.dh[block, :].astype(BF16)

        loop(4, rows)

    dq = r.dctx
    loads["H"].wait()
    dq[...] = r.qcot[...].astype(BF16)

    def top(i):
        lanes = span(i, 256)
        r.wide_tmp[:, lanes] = nn(dq[...], r.wH[:, lanes])

    loop(4, top)
    norm_back(r.h.at[2], 4, lambda block: r.wide_tmp[block, :], False)

    def head_grads():
        norm_into(r.h.at[2], 4, r.final)
        r.oe[0:256, :] = nt(r.final[...], r.wH[...])
        transposed(r.final)
        units = []
        for n in range(2):

            def write(value, n=n):
                r.oe[256:288, n * 128 : (n + 1) * 128] = value

            unit = share(n, True, n, write)
            outer(unit.g, nn(r.xt[:, 0:SEG], dq[:, n * 128 : (n + 1) * 128]))
            unit.advance()
            units.append(unit)
        return units

    def ffn_back(l, n):
        rounded_dh()

        def gate(i):
            lanes = span(i, 256)
            d_active = nn(r.dy[...], r.wD[l, :, lanes])
            r.dup[:, lanes] = (d_active * r.slope[l, :, lanes]).astype(BF16)

        loop(4, gate)
        return ar_begin(
            n, lambda base, i: nt(r.dup[at_rows(base), :], r.wU[l, span(i, 256), :])
        )

    def ffn_grads(l):
        units = []
        for kind, (left, right, out) in enumerate(
            ((r.dy, r.act.at[l], 1024), (r.b.at[l], r.dup, 0))
        ):
            transposed(left)
            for n in range(4):

                def write(value, base=out + n * 256):
                    r.oz[l, :, base : base + 256] = value

                units.append(
                    wide(
                        l * 12 + kind * 4 + n,
                        n,
                        lambda n=n, right=right: nn(
                            r.xt[:, 0:SEG], right[:, n * 256 : (n + 1) * 256]
                        ),
                        write,
                    )
                )
        return units

    def attention_back(l):
        norm_back(r.mid.at[l], 2 * l + 1, lambda block: r.db[block, :].astype(F32), True)
        rounded_dh()
        r.dctx[...] = nn(r.dy[...], r.wO[l]).astype(BF16)
        q, k, v = r.q.at[l], r.k.at[l], r.v.at[l]
        for head in range(2):
            lanes = slice(head * HD, (head + 1) * HD)
            d = r.dctx[:, lanes]
            probs = r.p[l, head]
            d_probs = nt(d, v[:, lanes])
            inner = jnp.sum(d_probs * probs, axis=-1, keepdims=True)
            d_scores = (probs * (d_probs - inner) * (HD**-0.5)).astype(BF16)
            r.dqs[:, lanes] = nn(d_scores, k[:, lanes]).astype(BF16)
            r.dkv[0, :, lanes] = tn(d_scores, q[:, lanes]).astype(BF16)
            r.dkv[1, :, lanes] = tn(probs.astype(BF16), d).astype(BF16)

    def unit_index(l, n):
        return l * 12 + 8 + n

    def out_grads(l):
        transposed(r.dy)

        def write(value):
            r.oz[l, :, 2048:2304] = value

        return [wide(unit_index(l, 3), 3, lambda: nn(r.xt[:, 0:SEG], r.ctx[l]), write)]

    def qkv_grads(l):
        transposed(r.a.at[l])
        units = []
        for n in range(3):

            def write(value, base=2304 + n * 256):
                r.oz[l, :, base : base + 256] = value

            def left(n=n):
                if n:
                    return nn(r.xt[...], r.dkv[n - 1])
                return nn(r.xt[:, SEG:], r.dqs[...])

            units.append(wide(unit_index(l, n), n, left, write))
        return units

    def back_part(l):
        def part(base, i):
            total = nt(r.dqs[at_rows(base), :], r.wA[l, 0, span(i, 256), :])
            for n in (1, 2):
                total = total + nt(
                    r.dkv[n - 1, at_rows(SEG + base), :], r.wA[l, n, span(i, 256), :]
                )
            return total

        return part

    copy = ffn_back(1, 4)
    ffn1 = ffn_grads(1)
    heads = head_grads()
    ar_end(4, copy, r.db, None)
    attention_back(1)
    copy = ar_begin(5, back_part(1))
    step(ffn1)
    step(heads)
    attn1 = out_grads(1) + qkv_grads(1)
    ar_end(5, copy, r.db, None)
    norm_back(r.h.at[1], 2, lambda block: r.db[block, :].astype(F32), True)
    copy = ffn_back(0, 6)
    step(ffn1)
    step(heads)
    step(attn1)
    ffn0 = ffn_grads(0)
    ar_end(6, copy, r.db, None)
    attention_back(0)
    attn0 = out_grads(0) + qkv_grads(0)
    step(heads)
    step(ffn1)
    step(attn1)

    def normal(i):
        block = span(i, 64)
        x = r.h[0, block, :].astype(F32)
        r.dh[block, :] = x * lax.rsqrt(jnp.mean(x * x, axis=-1, keepdims=True) + EPS)

    loop(4, normal)
    part = back_part(0)
    for half in range(2):

        def gain(i):
            lanes = span(i, 256)
            rows = pl.ds(half * 128, 128)
            value = part(half * 128, i) * r.dh[rows, lanes]
            r.gg[0, :, lanes] += jnp.sum(value.reshape(16, 8, 256), axis=0)

        loop(4, gain)
    copy = remote(r.gg.at[0], r.g0.at[0], r.g0_s.at[0], r.g0_r.at[0], beside)
    copy.start()
    copy.wait()
    r.g0s[...] = r.gg[0] + r.g0[0]
    copy = remote(r.g0s, r.g0.at[1], r.g0_s.at[1], r.g0_r.at[1], across)
    copy.start()
    step(heads)
    step(ffn1)
    step(attn1)
    step(ffn0)
    copy.wait()
    rows = [jnp.sum(r.g0s[...] + r.g0[1], axis=0, keepdims=True)]
    rows += [jnp.sum(r.gg[n], axis=0, keepdims=True) for n in range(1, 5)]
    table = jnp.concatenate(rows + [jnp.zeros((123, D), F32)], axis=0)

    def write_gains(value):
        r.oe[288:320, 0:128] = value

    unit = share(2, True, 3, write_gains)
    outer(unit.g, table.T)
    unit.advance()
    step(attn0)
    tail = attn0 + [unit]
    for n in range(2, 7):
        step(heads)
        step(ffn1)
        step(attn1)
        step(ffn0)
        step(tail)


def body(tokens, w_attn, w_out, w_up, w_down, w_head, gains, q_cotangent, bounds, resets):
    vmem = pl.BlockSpec(memory_space=pltpu.VMEM)
    smem = pl.BlockSpec(memory_space=pltpu.SMEM)
    anywhere = pl.BlockSpec(memory_space=pl.ANY)
    shapes = [(2, 32, 3072), (320, 256)]
    outs = pl.pallas_call(
        kernel,
        out_shape=[jax.ShapeDtypeStruct(shape, F32) for shape in shapes],
        in_specs=[anywhere] * 6 + [vmem] * 2 + [smem] * 2,
        out_specs=[vmem] * len(shapes),
        scratch_shapes=list(scratch().values()),
        compiler_params=pltpu.CompilerParams(
            collective_id=0, has_side_effects=True, vmem_limit_bytes=67043328
        ),
    )(
        tokens,
        jnp.transpose(w_attn, (0, 2, 1, 3)),
        w_out,
        w_up,
        w_down,
        w_head,
        gains,
        q_cotangent,
        bounds,
        resets,
    )
    grads, rest = outs
    return (
        rest[:256],
        grads[:, :, 2304:].reshape(2, 32, 3, 256),
        grads[:, :, 2048:2304],
        grads[:, :, :1024],
        grads[:, :, 1024:2048],
        rest[256:288].T,
        rest[288:320, :5].T,
    )


def solution(mesh):
    return jax.shard_map(
        body,
        mesh=mesh,
        in_specs=(
            P("seq", None),
            P(None, None, None, "tensor"),
            P(None, None, "tensor"),
            P(None, None, "tensor"),
            P(None, None, "tensor"),
            P(),
            P(),
            P("seq", None),
            P("seq"),
            P("seq"),
        ),
        out_specs=(
            P("seq", None),
            P(None, "seq", None, "tensor"),
            P(None, "seq", "tensor"),
            P(None, "seq", "tensor"),
            P(None, "seq", "tensor"),
            P(None, "seq"),
            P(None, "seq"),
        ),
        check_vma=False,
    )
```

profile of v0, /device:TPU:0, one launch (start us, length us, event | category | flops | bytes accessed | tf_op | source)
XLA Modules:
  0.0 187.6 jit_solution(7505289884204958146)
XLA Ops:
  1.9 176.3 %shard_map.153 = (f32[2,32,3072]{2,1,0:T(8,128)}, f32[320,256]{1,0:T(8,128)}) custom-call(bf16[256,1024]{1,0:T(8,128)(2,1)} %refs_0_.1, bf16[2,3,1024,256]{3,2,1,0:T(8,128)(2,1)} %bitcast.9, bf16[2,1024,256]{2,1,0:T(8,128)(2,1)} %refs_2_.1, bf16[2,1024,1024]{2,1,0:T(8,128)(2,1)} %refs_3_.1, bf16[2,1024,1024]{2,1,0:T(8,128)(2,1)} %refs_4_.1, ...), custom_call_target="tpu_custom_call" | custom-call | tf_op jit(solution)/shard_map/pallas_call | solution.py:679
  178.2 0.7 slice_bitcast_fusion.1
  178.9 0.7 copy.20
  179.6 1.4 slice_bitcast_fusion
  181.0 1.7 slice.21
  182.6 1.5 slice.23
  184.1 0.9 slice.22
  185.0 1.9 fusion
  186.9 0.7 copy.23
where the time goes:
time: 189 us; the launch traced here: 188 us
  Pallas kernels  176 us (93%)
  local copies, waits for them, and re-layouts  9.41 us (5%)
  between operations  1.94 us (1%)
    pallas_call x1, Pallas kernels, body(): pl.pallas_call(kernel, out_shape=[jax.ShapeDtypeStruct(shape, F32) for sh...  176 us

commit v1 on v0

--- a/solution.py
+++ b/solution.py
@@ -43,6 +43,8 @@
 
 
 def span(i, size):
+    if isinstance(i, int):
+        return pl.ds(i * size, size)
     return pl.ds(pl.multiple_of(i * size, size), size)
 
 
@@ -82,7 +84,6 @@
         ar_half=v((2, 128, D), BF16),
         ar_sum=v((128, D), BF16),
         ar_far=v((2, 128, D), BF16),
-        ar_own=v((128, D), F32),
         db=v((SEG, D), BF16),
         dh=v((SEG, D), F32),
         xt=v((D, 2 * SEG), BF16),
@@ -101,18 +102,15 @@
         G=v((UNITS, 2, 4, 4, 32, 256), BF16),
         R1=v((UNITS, 2, 2, 4, 32, 256), BF16),
         R2=v((UNITS, 2, 4, 32, 256), BF16),
-        R3=v((UNITS, 2, 2, 32, 256), BF16),
-        R4=v((UNITS, 2, 32, 256), BF16),
+        R3=v((UNITS, 3, 2, 32, 256), BF16),
         R5=v((UNITS, 32, 256), BF16),
         G_=v((NARROW, 2, 4, 4, 32, 128), BF16),
-        R1_=v((NARROW, 2, 2, 4, 32, 128), BF16),
-        R2_=v((NARROW, 2, 4, 32, 128), BF16),
-        R3_=v((NARROW, 2, 2, 32, 128), BF16),
-        R4_=v((NARROW, 2, 32, 128), BF16),
+        R1_=v((NARROW, 3, 2, 4, 32, 128), BF16),
+        R3_=v((NARROW, 3, 2, 32, 128), BF16),
         R5_=v((NARROW, 32, 128), BF16),
         w_sem=dma((10,)),
-        ar_s=dma((7, 3)),
-        ar_r=dma((7, 3)),
+        ar_s=dma((7, 12)),
+        ar_r=dma((7, 12)),
         kv_s=dma((2, 2)),
         kv_r=dma((2, 2)),
         pa_s=dma((2, 2)),
@@ -126,22 +124,23 @@
     )
 
 
-COLORS = (("y", 0, 0), ("z", 0, 0), ("y", 1, 1), ("z", 1, 1))
+COLORS = (("y", 0), ("z", 0), ("y", 1), ("z", 1))
 
 
 class Share:
     def __init__(self, r, here, index, narrow, color, write):
         tail = "_" if narrow else ""
-        self.g, self.r1, self.r2, self.r3, self.r4, self.r5 = (
-            getattr(r, name + tail).at[index] for name in ("G", "R1", "R2", "R3", "R4", "R5")
-        )
+        self.g, self.r1, self.r3, self.r5 = (
+            getattr(r, name + tail).at[index] for name in ("G", "R1", "R3", "R5")
+        )
+        self.narrow = narrow
+        self.r2 = None if narrow else r.R2.at[index]
         row = index + (UNITS if narrow else 0)
         self.ss = [r.rs_s.at[row, n] for n in range(7)]
         self.rs = [r.rs_r.at[row, n] for n in range(7)]
         self.here = here
-        self.axis, o1, o2 = color
+        self.axis, o1 = color
         self.f1, self.f2 = (far, near) if o1 else (near, far)
-        self.e1, self.e2 = (far, near) if o2 else (near, far)
         self.write = write
         self.stage = 0
 
@@ -175,13 +174,35 @@
         copy.start()
         return copy
 
+    def spread(self, n, view, target, to):
+        at = (self.here.y, self.here.z)[(self.axis == "z") == (n == 0)]
+        copies = []
+        for d in range(1, 4):
+            peer = lax.rem(at + d, 4)
+            copies.append(self.send(n + d - 1, view(peer), target.at[d - 1], to(peer)))
+        return copies
+
+    def gather(self, part, others):
+        total = part[...].astype(F32)
+        for other in others:
+            total = total + other[...].astype(F32)
+        return total
+
+    def fold(self, part, others):
+        part[...] = self.gather(part, others).astype(BF16)
+
     def advance(self):
         h = self.here
         v, w = (h.y, h.z) if self.axis == "y" else (h.z, h.y)
         stage = self.stage
-        if stage > 5:
+        if self.narrow and stage:
+            stage += 1
+        if stage > 4:
             return
         self.stage += 1
+        if stage == 0 and self.narrow:
+            self.c = self.spread(0, self.one, self.r1, lambda peer: self.device(first=peer))
+            return
         if stage == 0:
             peer = self.f1(v)
             to = self.device(first=peer)
@@ -195,34 +216,20 @@
         if stage == 1:
             peer = self.f2(v)
             part = self.one(peer)
-            part[...] = (part[...].astype(F32) + self.r1[1].astype(F32)).astype(BF16)
+            self.fold(part, [self.r1.at[1]])
             self.c = [self.send(2, part, self.r2, self.device(first=peer))]
         elif stage == 2:
-            part = self.one(v)
-            part[...] = (
-                part[...].astype(F32) + self.r1[0].astype(F32) + self.r2[...].astype(F32)
-            ).astype(BF16)
-            peer = self.e1(w)
-            to = self.device(second=peer)
-            self.c = [
-                self.send(3, self.two(peer), self.r3.at[0], to),
-                self.send(4, self.two(self.e2(peer)), self.r3.at[1], to),
-            ]
+            if self.narrow:
+                self.fold(self.one(v), [self.r1.at[d] for d in range(3)])
+            else:
+                self.fold(self.one(v), [self.r1.at[0], self.r2])
+            self.c = self.spread(3, self.two, self.r3, lambda peer: self.device(second=peer))
         elif stage == 3:
-            peer = self.e2(w)
-            part = self.two(peer)
-            part[...] = (part[...].astype(F32) + self.r3[1].astype(F32)).astype(BF16)
-            self.c = [self.send(5, part, self.r4, self.device(second=peer))]
-        elif stage == 4:
-            part = self.two(w)
-            part[...] = (
-                part[...].astype(F32) + self.r3[0].astype(F32) + self.r4[...].astype(F32)
-            ).astype(BF16)
+            self.fold(self.two(w), [self.r3.at[d] for d in range(3)])
             other = self.g.at[1 - h.x, h.y, h.z]
             self.c = [self.send(6, other, self.r5, self.device(x=1 - h.x))]
         else:
-            own = self.g[h.x, h.y, h.z]
-            self.write(own.astype(F32) + self.r5[...].astype(F32))
+            self.write(self.gather(self.g.at[h.x, h.y, h.z], [self.r5]))
 
 
 def norm_vjp(x, gain, dy):
@@ -257,6 +264,8 @@
         at(here.x, far(here.y), here.z),
         at(here.x, here.y, near(here.z)),
         at(here.x, here.y, far(here.z)),
+        at(here.x, lax.rem(here.y + 2, 4), here.z),
+        at(here.x, here.y, lax.rem(here.z + 2, 4)),
     ]
 
     loads = {}
@@ -300,40 +309,57 @@
         loop(4, rows)
 
     def ar_begin(n, part):
-        base = (1 - core) * 128
-
-        def first(i):
-            r.ar_send[:, span(i, 256)] = part(base, i).astype(BF16)
-
-        loop(4, first)
-        half = r.ar_half.at[n % 2]
-        copy = remote(r.ar_send, half, r.ar_s.at[n, 0], r.ar_r.at[n, 0], beside)
-        copy.start()
-
-        def second(i):
-            r.ar_own[:, span(i, 256)] = part(core * 128, i)
-
-        loop(4, second)
-        copy.wait()
-        r.ar_sum[...] = (r.ar_own[...] + half[...].astype(F32)).astype(BF16)
-        copy = remote(
-            r.ar_sum, r.ar_far.at[n % 2], r.ar_s.at[n, 1], r.ar_r.at[n, 1], across
-        )
-        copy.start()
-        return copy
-
-    def ar_end(n, copy, target, residual):
-        copy.wait()
+        half, distant = r.ar_half.at[n % 2], r.ar_far.at[n % 2]
+        near_copies, far_copies = [], []
+        for i in range(4):
+            lanes = slice(i * 256, (i + 1) * 256)
+            r.ar_send[:, lanes] = part((1 - core) * 128, i).astype(BF16)
+            copy = remote(
+                r.ar_send.at[:, lanes],
+                half.at[:, lanes],
+                r.ar_s.at[n, i],
+                r.ar_r.at[n, i],
+                beside,
+            )
+            copy.start()
+            near_copies.append(copy)
+        for i in range(4):
+            lanes = slice(i * 256, (i + 1) * 256)
+            mine = part(core * 128, i)
+            near_copies[i].wait()
+            r.ar_sum[:, lanes] = (mine + half[:, lanes].astype(F32)).astype(BF16)
+            copy = remote(
+                r.ar_sum.at[:, lanes],
+                distant.at[:, lanes],
+                r.ar_s.at[n, 4 + i],
+                r.ar_r.at[n, 4 + i],
+                across,
+            )
+            copy.start()
+            far_copies.append(copy)
+        return far_copies
+
+    def ar_end(n, far_copies, target, residual):
         mine = pl.ds(pl.multiple_of(core * 128, 128), 128)
-        total = r.ar_sum[...].astype(F32) + r.ar_far[n % 2].astype(F32)
-        if residual is not None:
-            total = residual[mine, :].astype(F32) + total
-        target[mine, :] = total.astype(BF16)
-        copy = remote(
-            target.at[mine, :], target.at[mine, :], r.ar_s.at[n, 2], r.ar_r.at[n, 2], beside
-        )
-        copy.start()
-        copy.wait()
+        copies = []
+        for i in range(4):
+            lanes = slice(i * 256, (i + 1) * 256)
+            far_copies[i].wait()
+            total = r.ar_sum[:, lanes].astype(F32) + r.ar_far[n % 2, :, lanes].astype(F32)
+            if residual is not None:
+                total = residual[mine, lanes].astype(F32) + total
+            target[mine, lanes] = total.astype(BF16)
+            copy = remote(
+                target.at[mine, lanes],
+                target.at[mine, lanes],
+                r.ar_s.at[n, 8 + i],
+                r.ar_r.at[n, 8 + i],
+                beside,
+            )
+            copy.start()
+            copies.append(copy)
+        for copy in copies:
+            copy.wait()
 
     def at_rows(base):
         return pl.ds(pl.multiple_of(base, 128), 128)
@@ -642,14 +668,13 @@
         loop(4, gain)
     copy = remote(r.gg.at[0], r.g0.at[0], r.g0_s.at[0], r.g0_r.at[0], beside)
     copy.start()
+    down0, up0 = ffn0[:4], ffn0[4:]
+    step(down0)
     copy.wait()
     r.g0s[...] = r.gg[0] + r.g0[0]
     copy = remote(r.g0s, r.g0.at[1], r.g0_s.at[1], r.g0_r.at[1], across)
     copy.start()
-    step(heads)
-    step(ffn1)
-    step(attn1)
-    step(ffn0)
+    step(up0)
     copy.wait()
     rows = [jnp.sum(r.g0s[...] + r.g0[1], axis=0, keepdims=True)]
     rows += [jnp.sum(r.gg[n], axis=0, keepdims=True) for n in range(1, 5)]
@@ -661,14 +686,34 @@
     unit = share(2, True, 3, write_gains)
     outer(unit.g, table.T)
     unit.advance()
+    gain0 = [unit]
+    step(ffn1)
+    step(attn1)
+    step(down0)
     step(attn0)
-    tail = attn0 + [unit]
-    for n in range(2, 7):
-        step(heads)
-        step(ffn1)
-        step(attn1)
-        step(ffn0)
-        step(tail)
+    step(up0)
+    step(gain0)
+    step(attn1)
+    step(down0)
+    step(attn0)
+    step(up0)
+    step(gain0)
+    step(down0)
+    step(attn0)
+    step(up0)
+    step(gain0)
+    step(attn0)
+
+
+def finish(oz, oe, values, attn, out, up, down, head, gains):
+    values[...] = oe[0:256, :]
+    for n in range(3):
+        attn[:, n] = oz[:, :, 2304 + n * 256 : 2560 + n * 256]
+    out[...] = oz[:, :, 2048:2304]
+    up[...] = oz[:, :, 0:1024]
+    down[...] = oz[:, :, 1024:2048]
+    head[...] = oe[256:288, :]
+    gains[...] = oe[288:320, 0:128].T[0:5, :]
 
 
 def body(tokens, w_attn, w_out, w_up, w_down, w_head, gains, q_cotangent, bounds, resets):
@@ -697,16 +742,22 @@
         bounds,
         resets,
     )
-    grads, rest = outs
-    return (
-        rest[:256],
-        grads[:, :, 2304:].reshape(2, 32, 3, 256),
-        grads[:, :, 2048:2304],
-        grads[:, :, :1024],
-        grads[:, :, 1024:2048],
-        rest[256:288].T,
-        rest[288:320, :5].T,
-    )
+    shapes = [
+        (256, 256),
+        (2, 3, 32, 256),
+        (2, 32, 256),
+        (2, 32, D),
+        (2, 32, D),
+        (32, 256),
+        (5, 32),
+    ]
+    values, attn, out, up, down, head, gain = pl.pallas_call(
+        finish,
+        out_shape=[jax.ShapeDtypeStruct(shape, F32) for shape in shapes],
+        in_specs=[vmem] * 2,
+        out_specs=[vmem] * len(shapes),
+    )(*outs)
+    return (values, jnp.transpose(attn, (0, 2, 1, 3)), out, up, down, head.T, gain)
 
 
 def solution(mesh):

time: 189 us -> 178 us (0.942)
  local copies, waits for them, and re-layouts: 9.41 us -> 0 us
    slice x4 -> x0, local copies, waits for them, and re-layouts: 5.95 us -> none  [the longest x1 1.87 us: body(): grads[:, :, 1024:2048]]
    pallas_call x1, Pallas kernels: 176 us -> 173 us  [body(): pl.pallas_call(kernel, out_shape=[jax.ShapeDtypeStruct(shape, F32) for sh...]
    pallas_call x0 -> x1, Pallas kernels: none -> 2.2 us  [body(): pl.pallas_call(finish, out_shape=[jax.ShapeDtypeStruct(shape, F32) for sh...]
    transpose x2 -> x0, local copies, waits for them, and re-layouts: 2.09 us -> none  [the longest x1 1.37 us: body(): rest[256:288]]
where the time goes in v1:
time: 178 us; the launch traced here: 177 us
  Pallas kernels  176 us (99%)
  between operations  1.94 us (1%)
    pallas_call x1, Pallas kernels, body(): pl.pallas_call(kernel, out_shape=[jax.ShapeDtypeStruct(shape, F32) for sh...  173 us

profile of v1, /device:TPU:0, one launch (start us, length us, event | category | flops | bytes accessed | tf_op | source)
XLA Modules:
  0.0 177.5 jit_solution(1989150947918938167)
XLA Ops:
  1.9 173.3 %shard_map.153 = (f32[2,32,3072]{2,1,0:T(8,128)}, f32[320,256]{1,0:T(8,128)}) custom-call(bf16[256,1024]{1,0:T(8,128)(2,1)} %refs_0_.1, bf16[2,3,1024,256]{3,2,1,0:T(8,128)(2,1)} %bitcast.3, bf16[2,1024,256]{2,1,0:T(8,128)(2,1)} %refs_2_.1, bf16[2,1024,1024]{2,1,0:T(8,128)(2,1)} %refs_3_.1, bf16[2,1024,1024]{2,1,0:T(8,128)(2,1)} %refs_4_.1, ...), custom_call_target="tpu_custom_call" | custom-call | tf_op jit(solution)/shard_map/pallas_call | solution.py:724
  175.3 2.2 %shard_map.154 = (f32[256,256]{1,0:T(8,128)}, f32[2,3,32,256]{3,2,1,0:T(8,128)}, f32[2,32,256]{2,1,0:T(8,128)}, f32[2,32,1024]{2,1,0:T(8,128)}, f32[2,32,1024]{2...) custom-call(f32[2,32,3072]{2,1,0:T(8,128)} %get-tuple-element.16.oz, f32[320,256]{1,0:T(8,128)} %get-tuple-element.17.oe), custom_call_target="tpu_custom_call" | custom-call | tf_op jit(solution)/shard_map/pallas_call | solution.py:754

commit v2 on v1

--- a/solution.py
+++ b/solution.py
@@ -19,7 +19,7 @@
 ROOT = 0.7978845608028654
 MESH = pl.DeviceIdType.MESH
 UNITS = 24
-NARROW = 3
+NARROW = 2
 
 
 def nn(a, b):
@@ -115,6 +115,9 @@
         kv_r=dma((2, 2)),
         pa_s=dma((2, 2)),
         pa_r=dma((2, 2)),
+        hx=v((2, 32, 128), F32),
+        hx_s=dma,
+        hx_r=dma,
         b_s=dma,
         b_r=dma,
         g0_s=dma((2,)),
@@ -310,8 +313,9 @@
 
     def ar_begin(n, part):
         half, distant = r.ar_half.at[n % 2], r.ar_far.at[n % 2]
-        near_copies, far_copies = [], []
-        for i in range(4):
+        near_copies, far_copies, own_parts = [], [], []
+
+        def give(i):
             lanes = slice(i * 256, (i + 1) * 256)
             r.ar_send[:, lanes] = part((1 - core) * 128, i).astype(BF16)
             copy = remote(
@@ -323,11 +327,14 @@
             )
             copy.start()
             near_copies.append(copy)
-        for i in range(4):
+
+        def keep(i):
+            own_parts.append(part(core * 128, i))
+
+        def pass_on(i):
             lanes = slice(i * 256, (i + 1) * 256)
-            mine = part(core * 128, i)
             near_copies[i].wait()
-            r.ar_sum[:, lanes] = (mine + half[:, lanes].astype(F32)).astype(BF16)
+            r.ar_sum[:, lanes] = (own_parts[i] + half[:, lanes].astype(F32)).astype(BF16)
             copy = remote(
                 r.ar_sum.at[:, lanes],
                 distant.at[:, lanes],
@@ -337,6 +344,19 @@
             )
             copy.start()
             far_copies.append(copy)
+
+        give(0)
+        give(1)
+        keep(0)
+        give(2)
+        pass_on(0)
+        keep(1)
+        give(3)
+        pass_on(1)
+        keep(2)
+        pass_on(2)
+        keep(3)
+        pass_on(3)
         return far_copies
 
     def ar_end(n, far_copies, target, residual):
@@ -525,20 +545,25 @@
         norm_into(r.h.at[2], 4, r.final)
         r.oe[0:256, :] = nt(r.final[...], r.wH[...])
         transposed(r.final)
-        units = []
-        for n in range(2):
-
-            def write(value, n=n):
-                r.oe[256:288, n * 128 : (n + 1) * 128] = value
-
-            unit = share(n, True, n, write)
-            outer(unit.g, nn(r.xt[:, 0:SEG], dq[:, n * 128 : (n + 1) * 128]))
-            unit.advance()
-            units.append(unit)
-        return units
-
-    def ffn_back(l, n):
+        r.hx_copy = remote(r.hx.at[0], r.hx.at[1], r.hx_s, r.hx_r, beside)
+
+        def write(value):
+            r.hx[0] = value
+            r.hx_copy.start()
+
+        unit = share(0, True, 0, write)
+        outer(unit.g, nn(r.xt[:, 0:SEG], dq[:, span(core, 128)]))
+        unit.advance()
+        return [unit]
+
+    def head_done():
+        r.hx_copy.wait()
+        r.oe[256:288, span(core, 128)] = r.hx[0]
+        r.oe[256:288, span(1 - core, 128)] = r.hx[1]
+
+    def ffn_back(l, n, early=False):
         rounded_dh()
+        down = ffn_kind(l, 0) if early else []
 
         def gate(i):
             lanes = span(i, 256)
@@ -546,31 +571,23 @@
             r.dup[:, lanes] = (d_active * r.slope[l, :, lanes]).astype(BF16)
 
         loop(4, gate)
-        return ar_begin(
+        return down, ar_begin(
             n, lambda base, i: nt(r.dup[at_rows(base), :], r.wU[l, span(i, 256), :])
         )
 
-    def ffn_grads(l):
+    def ffn_kind(l, kind):
+        left, right, out = ((r.dy, r.act.at[l], 1024), (r.b.at[l], r.dup, 0))[kind]
+        transposed(left)
         units = []
-        for kind, (left, right, out) in enumerate(
-            ((r.dy, r.act.at[l], 1024), (r.b.at[l], r.dup, 0))
-        ):
-            transposed(left)
-            for n in range(4):
-
-                def write(value, base=out + n * 256):
-                    r.oz[l, :, base : base + 256] = value
-
-                units.append(
-                    wide(
-                        l * 12 + kind * 4 + n,
-                        n,
-                        lambda n=n, right=right: nn(
-                            r.xt[:, 0:SEG], right[:, n * 256 : (n + 1) * 256]
-                        ),
-                        write,
-                    )
-                )
+        for n in range(4):
+
+            def write(value, base=out + n * 256):
+                r.oz[l, :, base : base + 256] = value
+
+            def block(n=n):
+                return nn(r.xt[:, 0:SEG], right[:, n * 256 : (n + 1) * 256])
+
+            units.append(wide(l * 12 + kind * 4 + n, n, block, write))
         return units
 
     def attention_back(l):
@@ -627,28 +644,30 @@
 
         return part
 
-    copy = ffn_back(1, 4)
-    ffn1 = ffn_grads(1)
+    down1, copy = ffn_back(1, 4, True)
+    up1 = ffn_kind(1, 1)
     heads = head_grads()
+    step(down1)
     ar_end(4, copy, r.db, None)
     attention_back(1)
     copy = ar_begin(5, back_part(1))
-    step(ffn1)
+    attn1 = out_grads(1) + qkv_grads(1)
+    step(up1)
+    step(down1)
     step(heads)
-    attn1 = out_grads(1) + qkv_grads(1)
     ar_end(5, copy, r.db, None)
     norm_back(r.h.at[1], 2, lambda block: r.db[block, :].astype(F32), True)
-    copy = ffn_back(0, 6)
-    step(ffn1)
+    _, copy = ffn_back(0, 6)
+    down0 = ffn_kind(0, 0)
+    up0 = ffn_kind(0, 1)
+    step(up1)
+    step(attn1)
     step(heads)
-    step(attn1)
-    ffn0 = ffn_grads(0)
     ar_end(6, copy, r.db, None)
     attention_back(0)
     attn0 = out_grads(0) + qkv_grads(0)
+    step(down1)
     step(heads)
-    step(ffn1)
-    step(attn1)
 
     def normal(i):
         block = span(i, 64)
@@ -668,12 +687,13 @@
         loop(4, gain)
     copy = remote(r.gg.at[0], r.g0.at[0], r.g0_s.at[0], r.g0_r.at[0], beside)
     copy.start()
-    down0, up0 = ffn0[:4], ffn0[4:]
     step(down0)
     copy.wait()
     r.g0s[...] = r.gg[0] + r.g0[0]
     copy = remote(r.g0s, r.g0.at[1], r.g0_s.at[1], r.g0_r.at[1], across)
     copy.start()
+    step(attn1)
+    step(up1)
     step(up0)
     copy.wait()
     rows = [jnp.sum(r.g0s[...] + r.g0[1], axis=0, keepdims=True)]
@@ -683,25 +703,27 @@
     def write_gains(value):
         r.oe[288:320, 0:128] = value
 
-    unit = share(2, True, 3, write_gains)
+    unit = share(1, True, 3, write_gains)
     outer(unit.g, table.T)
     unit.advance()
     gain0 = [unit]
-    step(ffn1)
-    step(attn1)
+    step(down1)
     step(down0)
     step(attn0)
+    step(up1)
+    step(attn1)
     step(up0)
     step(gain0)
-    step(attn1)
     step(down0)
     step(attn0)
+    step(attn1)
     step(up0)
     step(gain0)
     step(down0)
     step(attn0)
     step(up0)
     step(gain0)
+    head_done()
     step(attn0)
 
 

time: 178 us -> 176 us (0.989)
  Pallas kernels: 176 us -> 174 us
    pallas_call x1, Pallas kernels: 173 us -> 171 us  [body(): pl.pallas_call(kernel, out_shape=[jax.ShapeDtypeStruct(shape, F32) for sh...]
where the time goes in v2:
time: 176 us; the launch traced here: 175 us
  Pallas kernels  174 us (99%)
  between operations  1.94 us (1%)
    pallas_call x1, Pallas kernels, body(): pl.pallas_call(kernel, out_shape=[jax.ShapeDtypeStruct(shape, F32) for sh...  171 us

profile of v2, /device:TPU:0, one launch (start us, length us, event | category | flops | bytes accessed | tf_op | source)
XLA Modules:
  0.0 175.5 jit_solution(12895015310079499317)
XLA Ops:
  1.9 171.3 %shard_map.153 = (f32[2,32,3072]{2,1,0:T(8,128)}, f32[320,256]{1,0:T(8,128)}) custom-call(bf16[256,1024]{1,0:T(8,128)(2,1)} %refs_0_.1, bf16[2,3,1024,256]{3,2,1,0:T(8,128)(2,1)} %bitcast.3, bf16[2,1024,256]{2,1,0:T(8,128)(2,1)} %refs_2_.1, bf16[2,1024,1024]{2,1,0:T(8,128)(2,1)} %refs_3_.1, bf16[2,1024,1024]{2,1,0:T(8,128)(2,1)} %refs_4_.1, ...), custom_call_target="tpu_custom_call" | custom-call | tf_op jit(solution)/shard_map/pallas_call | solution.py:746
  173.3 2.2 %shard_map.154 = (f32[256,256]{1,0:T(8,128)}, f32[2,3,32,256]{3,2,1,0:T(8,128)}, f32[2,32,256]{2,1,0:T(8,128)}, f32[2,32,1024]{2,1,0:T(8,128)}, f32[2,32,1024]{2...) custom-call(f32[2,32,3072]{2,1,0:T(8,128)} %get-tuple-element.16.oz, f32[320,256]{1,0:T(8,128)} %get-tuple-element.17.oe), custom_call_target="tpu_custom_call" | custom-call | tf_op jit(solution)/shard_map/pallas_call | solution.py:776

commit v3 on v2

--- a/solution.py
+++ b/solution.py
@@ -657,16 +657,18 @@
     step(heads)
     ar_end(5, copy, r.db, None)
     norm_back(r.h.at[1], 2, lambda block: r.db[block, :].astype(F32), True)
-    _, copy = ffn_back(0, 6)
-    down0 = ffn_kind(0, 0)
-    up0 = ffn_kind(0, 1)
+    down0, copy = ffn_back(0, 6, True)
     step(up1)
     step(attn1)
     step(heads)
+    up0 = ffn_kind(0, 1)
     ar_end(6, copy, r.db, None)
+    step(down1)
+    step(up1)
+    step(attn1)
     attention_back(0)
     attn0 = out_grads(0) + qkv_grads(0)
-    step(down1)
+    step(down0)
     step(heads)
 
     def normal(i):
@@ -687,13 +689,10 @@
         loop(4, gain)
     copy = remote(r.gg.at[0], r.g0.at[0], r.g0_s.at[0], r.g0_r.at[0], beside)
     copy.start()
-    step(down0)
     copy.wait()
     r.g0s[...] = r.gg[0] + r.g0[0]
     copy = remote(r.g0s, r.g0.at[1], r.g0_s.at[1], r.g0_r.at[1], across)
     copy.start()
-    step(attn1)
-    step(up1)
     step(up0)
     copy.wait()
     rows = [jnp.sum(r.g0s[...] + r.g0[1], axis=0, keepdims=True)]
@@ -708,15 +707,15 @@
     unit.advance()
     gain0 = [unit]
     step(down1)
+    step(up1)
+    step(attn1)
     step(down0)
     step(attn0)
-    step(up1)
-    step(attn1)
     step(up0)
     step(gain0)
+    step(attn1)
     step(down0)
     step(attn0)
-    step(attn1)
     step(up0)
     step(gain0)
     step(down0)

time: 176 us -> 173 us (0.983)
  Pallas kernels: 174 us -> 171 us
    pallas_call x1, Pallas kernels: 171 us -> 168 us  [body(): pl.pallas_call(kernel, out_shape=[jax.ShapeDtypeStruct(shape, F32) for sh...]
where the time goes in v3:
time: 173 us
  Pallas kernels  171 us (99%)
  between operations  1.94 us (1%)
    pallas_call x1, Pallas kernels, body(): pl.pallas_call(kernel, out_shape=[jax.ShapeDtypeStruct(shape, F32) for sh...  168 us

profile of v3, /device:TPU:0, one launch (start us, length us, event | category | flops | bytes accessed | tf_op | source)
XLA Modules:
  0.0 172.5 jit_solution(1024905250332835701)
XLA Ops:
  1.9 168.4 %shard_map.153 = (f32[2,32,3072]{2,1,0:T(8,128)}, f32[320,256]{1,0:T(8,128)}) custom-call(bf16[256,1024]{1,0:T(8,128)(2,1)} %refs_0_.1, bf16[2,3,1024,256]{3,2,1,0:T(8,128)(2,1)} %bitcast.3, bf16[2,1024,256]{2,1,0:T(8,128)(2,1)} %refs_2_.1, bf16[2,1024,1024]{2,1,0:T(8,128)(2,1)} %refs_3_.1, bf16[2,1024,1024]{2,1,0:T(8,128)(2,1)} %refs_4_.1, ...), custom_call_target="tpu_custom_call" | custom-call | tf_op jit(solution)/shard_map/pallas_call | solution.py:745
  170.3 2.2 %shard_map.154 = (f32[256,256]{1,0:T(8,128)}, f32[2,3,32,256]{3,2,1,0:T(8,128)}, f32[2,32,256]{2,1,0:T(8,128)}, f32[2,32,1024]{2,1,0:T(8,128)}, f32[2,32,1024]{2...) custom-call(f32[2,32,3072]{2,1,0:T(8,128)} %get-tuple-element.16.oz, f32[320,256]{1,0:T(8,128)} %get-tuple-element.17.oe), custom_call_target="tpu_custom_call" | custom-call | tf_op jit(solution)/shard_map/pallas_call | solution.py:775
